TPU v7x, 32 devices: a 4x4x1 block of a 4x4x8 slice. The times are simulated.
32 devices in a mesh: dp: 1 (over z), tp: 4 (over y), sp: 8 (over x, core).
Axes of the slice: x: 4, y: 4, z: 1, core: 2. Of those that a mesh axis runs over, the one named last changes fastest.
The devices are a block of a 4x4x8 slice.
Arguments:
- layer_in: bfloat16 [128, 6144], P('dp')
- new_pos: int32 [128], P('dp')
- k_cache: bfloat16 [128, 512, 8, 128], P('dp', 'sp', 'tp')
- v_cache: bfloat16 [128, 512, 8, 128], P('dp', 'sp', 'tp')
- attn_gain: bfloat16 [6144], replicated
- w_query: bfloat16 [6144, 6144], P(None, 'tp')
- w_key: bfloat16 [6144, 1024], P(None, 'tp')
- w_value: bfloat16 [6144, 1024], P(None, 'tp')
- w_out: bfloat16 [6144, 6144], P('tp')
- mlp_gain: bfloat16 [6144], replicated
- w_gate: bfloat16 [6144, 16384], P(None, 'tp')
- w_up: bfloat16 [6144, 16384], P(None, 'tp')
- w_down: bfloat16 [16384, 6144], P('tp')
Outputs:
- output 1: bfloat16 [128, 6144], P('dp')
- output 2: bfloat16 [128, 512, 8, 128], P('dp', 'sp', 'tp')
- output 3: bfloat16 [128, 512, 8, 128], P('dp', 'sp', 'tp')
- output 4: bfloat16 [128, 8, 128], P('dp', 'tp')
- output 5: bfloat16 [128, 8, 128], P('dp', 'tp')
All inputs are finite; a program needn't handle non-finite values.
Results may differ from a plain program's by a relative error of at most 0.00516591.
Values sent between devices are 32-bit elements.
A program may use at most 768 MiB of HBM per device.

v0:
```python
import jax
import jax.numpy as jnp
from jax import lax
from jax.sharding import PartitionSpec as P

ROPE_THETA = 1000000


def rms_norm(in_vec, gain_vec):
    mean_sq = jnp.mean(jnp.square(in_vec), axis=-1, keepdims=True)
    return in_vec * lax.rsqrt(mean_sq + 1e-5) * gain_vec.astype(jnp.float32)


def apply_rotary(in_vec, positions):
    head_dim = in_vec.shape[-1]
    half_idx = jnp.arange(head_dim // 2, dtype=jnp.float32)
    inv_freq = 1.0 / (ROPE_THETA ** (2.0 * half_idx / head_dim))
    angles = positions.astype(jnp.float32)[:, None] * inv_freq[None, :]
    cos_a = jnp.cos(angles)[:, None, :]
    sin_a = jnp.sin(angles)[:, None, :]
    pair_view = in_vec.reshape(in_vec.shape[:-1] + (head_dim // 2, 2))
    even_part = pair_view[..., 0]
    odd_part = pair_view[..., 1]
    rotated = jnp.stack([even_part * cos_a - odd_part * sin_a, even_part * sin_a + odd_part * cos_a], axis=-1)
    return rotated.reshape(in_vec.shape)


def solution(mesh):
    def local_step(layer_in, new_pos, k_blk, v_blk, attn_gain, w_query, w_key, w_value, w_out, mlp_gain, w_gate, w_up, w_down):
        num_rows = layer_in.shape[0]
        blk_len = k_blk.shape[1]
        kv_loc = k_blk.shape[2]
        head_dim = k_blk.shape[3]
        heads_loc = w_query.shape[1] // head_dim
        group_size = heads_loc // kv_loc
        x_f32 = layer_in.astype(jnp.float32)
        normed = rms_norm(x_f32, attn_gain).astype(jnp.bfloat16)
        q_proj = jnp.dot(normed, w_query, preferred_element_type=jnp.float32).reshape(num_rows, heads_loc, head_dim)
        k_proj = jnp.dot(normed, w_key, preferred_element_type=jnp.float32).reshape(num_rows, kv_loc, head_dim)
        v_new = jnp.dot(normed, w_value, preferred_element_type=jnp.float32).reshape(num_rows, kv_loc, head_dim).astype(jnp.bfloat16)
        q_rot = apply_rotary(q_proj, new_pos).astype(jnp.bfloat16)
        k_rot = apply_rotary(k_proj, new_pos).astype(jnp.bfloat16)
        slot_ids = lax.axis_index('sp') * blk_len + jnp.arange(blk_len)
        is_new = (slot_ids[None, :] == new_pos[:, None])[:, :, None, None]
        k_upd = jnp.where(is_new, k_rot[:, None], k_blk)
        v_upd = jnp.where(is_new, v_new[:, None], v_blk)
        q_grp = q_rot.reshape(num_rows, kv_loc, group_size, head_dim)
        scores = jnp.einsum('bkgd,bskd->bkgs', q_grp, k_upd, preferred_element_type=jnp.float32) * (head_dim ** -0.5)
        is_valid = (slot_ids[None, :] <= new_pos[:, None])[:, None, None, :]
        scores = jnp.where(is_valid, scores, -jnp.inf)
        row_max = lax.pmax(jnp.max(scores, axis=-1, keepdims=True), 'sp')
        prob_vals = jnp.exp(scores - row_max)
        denom_sum = lax.psum(jnp.sum(prob_vals, axis=-1, keepdims=True), 'sp')
        part_vals = jnp.einsum('bkgs,bskd->bkgd', prob_vals.astype(jnp.bfloat16), v_upd, preferred_element_type=jnp.float32)
        weighted = lax.psum(part_vals, 'sp')
        attn_vec = (weighted / denom_sum).reshape(num_rows, heads_loc * head_dim).astype(jnp.bfloat16)
        hidden = x_f32 + lax.psum(jnp.dot(attn_vec, w_out, preferred_element_type=jnp.float32), 'tp')
        normed_mlp = rms_norm(hidden, mlp_gain).astype(jnp.bfloat16)
        gate_pre = jnp.dot(normed_mlp, w_gate, preferred_element_type=jnp.float32)
        up_proj = jnp.dot(normed_mlp, w_up, preferred_element_type=jnp.float32)
        act_bf = (jax.nn.silu(gate_pre) * up_proj).astype(jnp.bfloat16)
        mlp_part = jnp.dot(act_bf, w_down, preferred_element_type=jnp.float32)
        layer_out = (hidden + lax.psum(mlp_part, 'tp')).astype(jnp.bfloat16)
        return layer_out, k_upd, v_upd, k_rot, v_new

    cache_spec = P('dp', 'sp', 'tp', None)
    new_spec = P('dp', 'tp', None)
    in_specs = (P('dp', None), P('dp'), cache_spec, cache_spec, P(None), P(None, 'tp'), P(None, 'tp'), P(None, 'tp'), P('tp', None), P(None), P(None, 'tp'), P(None, 'tp'), P('tp', None))
    out_specs = (P('dp', None), cache_spec, cache_spec, new_spec, new_spec)
    return jax.shard_map(local_step, mesh=mesh, in_specs=in_specs, out_specs=out_specs, check_vma=False)
```

profile of v0, /device:TPU:97, one launch (start us, length us, event | category | flops | bytes accessed | tf_op | source)
XLA Modules:
  0.0 368.6 jit_solution(14610993251567619208)
XLA Ops:
  7.2 0.0 copy-start
  7.2 0.1 all-reduce.4.cloned.1.call-start
  7.3 0.8 convert_element_type.60
  8.1 1.8 fusion.6
  10.0 0.7 convert_element_type.58
  10.7 0.7 broadcast_compare_fusion.1
  11.4 0.0 copy-done
  11.4 2.0 convolution_convert_fusion
  13.5 0.0 copy-start.2
  13.5 0.0 copy-start.5
  13.5 3.9 %fusion.27 = f32[128,256]{0,1:T(8,128)S(1)} fusion(bf16[6144,256]{1,0:T(8,128)(2,1)} %param.19, bf16[128,6144]{1,0:T(8,128)(2,1)} %param.13, f32[6144]{0:T(1024)S(1)} %convert_element_type.58, f32[128]{0:T(128)S(1)} %add_rsqrt_fusion.1), kind=kOutput, calls=%fused_computation.47 | convolution fusion | flops 405798912 | bytes 4874752 | tf_op jit(solution)/shard_map/dot_general | solution.py:39
  17.4 0.2 multiply_cosine_fusion
  17.6 0.2 subtract_convert_fusion.1
  17.8 0.2 pad_maximum_fusion.1
  17.9 0.1 copy.22
  18.1 0.0 copy-done.2
  18.1 0.0 copy-start.6
  18.1 11.5 %fusion.29 = f32[128,1536]{0,1:T(8,128)S(1)} fusion(bf16[6144,1536]{1,0:T(8,128)(2,1)} %param.18, bf16[128,6144]{1,0:T(8,128)(2,1)S(1)} %copy-done.2, f32[6144]{0:T(1024)S(1)} %convert_element_type.58, f32[128]{0:T(128)S(1)} %add_rsqrt_fusion.1), kind=kOutput, calls=%fused_computation.48 | convolution fusion | flops 2419064832 | bytes 21258752 | tf_op jit(solution)/shard_map/dot_general | solution.py:38
  29.6 1.0 subtract_convert_fusion
  30.6 0.9 pad_maximum_fusion
  31.5 0.4 copy.23
  31.9 0.0 copy-done.5
  32.0 0.0 copy-done.6
  32.0 14.1 %broadcast_select_fusion.1 = (bf16[128,64,2,128]{3,2,1,0:T(2,128)(2,1)S(1)}, bf16[128,64,2,128]{3,2,1,0:T(2,128)(2,1)}) fusion(bf16[128,64,2,128]{3,2,1,0:T(2,128)(2,1)} %param.15, pred[128,64]{1,0:T(8,128)(4,1)S(1)} %get-tuple-element.17, bf16[128,2,128]{2,1,0:T(2,128)(2,1)S(1)} %copy.22, bf16[128,64,2,128]{3,2,1,0:T(2,128)(2,1)} %param.16, ...), kind=kLoop, calls=%fused_computation.1 | loop fusion | flops 4194304 | bytes 16916480 | tf_op jit(solution)/shard_map/jit(_where)/select_n | solution.py:45
  46.1 0.0 copy-start.4
  46.1 2.0 copy-done.4
  48.1 2.5 fusion.31
  50.6 25.4 %pmax.7 = f32[128,2,6]{2,1,0:T(2,128)S(1)} all-reduce(f32[128,2,6]{2,1,0:T(2,128)S(1)} %get-tuple-element.20), channel_id=1, replica_groups=mesh['dp'=1,'tp'=4,'sp'=8] {'sp'}, use_global_device_ids=true, to_apply=%region_2.3 | all-reduce | flops 1536 | bytes 12288 | tf_op jit(solution)/shard_map/pmax | solution.py:51
  76.1 4.4 %fusion.2 = f32[128,2,6,128]{3,2,1,0:T(8,128)} fusion(bf16[128,64,2,128]{3,2,1,0:T(2,128)(2,1)} %get-tuple-element.15, f32[128,2,6,64]{3,2,1,0:T(8,128)S(1)} %get-tuple-element.21, f32[128,2,6]{2,1,0:T(2,128)S(1)} %pmax.7), kind=kOutput, calls=%fused_computation.8 | convolution fusion | flops 25362432 | bytes 5380096 | tf_op jit(solution)/shard_map/bkgs,bskd->bkgd/dot_general | solution.py:54
  80.5 0.1 all-reduce.4.cloned.1.call-update
  80.5 0.1 all-reduce.6.cloned.1.call-start
  80.6 0.8 fusion.21
  81.4 25.7 %psum.29 = f32[128,2,6]{2,1,0:T(2,128)S(1)} all-reduce(f32[128,2,6]{2,1,0:T(2,128)S(1)} %fusion.21), channel_id=1, replica_groups=mesh['dp'=1,'tp'=4,'sp'=8] {'sp'}, use_global_device_ids=true, to_apply=%region_5.6 | all-reduce | flops 1536 | bytes 12288 | tf_op jit(solution)/shard_map/psum | solution.py:53
  107.2 32.4 %all-reduce.4.cloned.1.call-done = f32[128,2,6,128]{3,2,1,0:T(8,128)} async-done(((f32[128,2,6,128]{3,2,1,0:T(8,128)}), f32[128,2,6,128]{3,2,1,0:T(8,128)}) %all-reduce.4.cloned.1.call-update) | async-done | bytes 786448 | tf_op jit(solution)/shard_map/psum | solution.py:55
  139.6 1.6 divide_convert_fusion
  141.1 0.4 copy.26
  141.5 10.8 %fusion.32 = f32[128,6144]{1,0:T(8,128)} fusion(bf16[128,1536]{0,1:T(8,128)(2,1)S(1)} %bitcast.25, bf16[1536,6144]{1,0:T(8,128)(2,1)} %param.21), kind=kOutput, calls=%fused_computation.50 | convolution fusion | flops 2415919104 | bytes 22413312 | tf_op jit(solution)/shard_map/dot_general | solution.py:57
  152.3 0.0 copy-start.7
  152.3 0.1 all-reduce.6.cloned.1.call-update
  152.4 0.1 all-reduce.8.cloned.1.call-start
  152.5 0.6 copy-done.7
  153.0 71.1 %all-reduce.6.cloned.1.call-done = f32[128,6144]{1,0:T(8,128)} async-done(((f32[128,6144]{1,0:T(8,128)}), f32[128,6144]{1,0:T(8,128)}) %all-reduce.6.cloned.1.call-update) | async-done | bytes 3145744 | tf_op jit(solution)/shard_map/psum | solution.py:57
  224.1 0.0 copy-start.3
  224.1 2.5 multiply_reduce_fusion
  226.6 0.3 copy-done.3
  226.9 0.5 multiply_convert_fusion
  227.5 19.3 %fusion.33 = f32[128,4096]{1,0:T(8,128)} fusion(bf16[128,6144]{1,0:T(8,128)(2,1)S(1)} %multiply_convert_fusion, bf16[6144,4096]{1,0:T(8,128)(2,1)} %param.23), kind=kOutput, calls=%fused_computation.51 | convolution fusion | flops 6442450944 | bytes 54001664 | tf_op jit(solution)/shard_map/dot_general | solution.py:59
  246.8 19.4 %fusion.clone.4 = bf16[128,4096]{1,0:T(8,128)(2,1)S(1)} fusion(bf16[128,6144]{1,0:T(8,128)(2,1)S(1)} %multiply_convert_fusion, bf16[6144,4096]{1,0:T(8,128)(2,1)} %param.24, f32[128,4096]{1,0:T(8,128)} %fusion.33), kind=kOutput, calls=%fused_computation.3.clone.clone.clone.1 | convolution fusion | flops 6445596672 | bytes 55050240 | tf_op jit(solution)/shard_map/dot_general | solution.py:60
  266.2 20.5 %fusion.1 = f32[128,6144]{1,0:T(8,128)} fusion(bf16[4096,6144]{1,0:T(8,128)(2,1)} %param.25, bf16[128,4096]{1,0:T(8,128)(2,1)S(1)} %fusion.clone.4), kind=kOutput, calls=%fused_computation.4 | convolution fusion | flops 6442450944 | bytes 54525952 | tf_op jit(solution)/shard_map/dot_general | solution.py:62
  286.7 0.1 all-reduce.8.cloned.1.call-update
  286.7 0.0 copy-start.1
  286.7 70.4 %all-reduce.8.cloned.1.call-done = f32[128,6144]{1,0:T(8,128)} async-done(((f32[128,6144]{1,0:T(8,128)}), f32[128,6144]{1,0:T(8,128)}) %all-reduce.8.cloned.1.call-update) | async-done | bytes 3145744 | tf_op jit(solution)/shard_map/psum | solution.py:63
  357.2 4.9 %add_convert_fusion = bf16[128,6144]{1,0:T(8,128)(2,1)} fusion(f32[128,6144]{1,0:T(8,128)} %all-reduce.8.cloned.1.call-done, f32[128,6144]{1,0:T(8,128)} %all-reduce.6.cloned.1.call-done, bf16[128,6144]{1,0:T(8,128)(2,1)} %param.13), kind=kLoop, calls=%fused_computation.15 | loop fusion | flops 3145728 | bytes 9437184 | tf_op jit(solution)/shard_map/convert_element_type | solution.py:63
  362.1 0.0 copy-done.1
  (6 shorter events, 0.1 us)
Async XLA Ops:
  7.2 4.2 %copy-start = (bf16[6144,256]{1,0:T(8,128)(2,1)S(1)}, bf16[6144,256]{1,0:T(8,128)(2,1)}, u32[]{:S(2)}) copy-start(bf16[6144,256]{1,0:T(8,128)(2,1)} %param.20) | copy-start | bytes 9437188
  7.2 132.4 %all-reduce.4.cloned.1.call-start = ((), (), s32[]{:S(2)}) async-start(), calls=%async_computation | async-start | bytes 2097152 | tf_op jit(solution)/shard_map/psum | solution.py:55
  13.5 4.6 %copy-start.2 = (bf16[128,6144]{1,0:T(8,128)(2,1)S(1)}, bf16[128,6144]{1,0:T(8,128)(2,1)}, u32[]{:S(2)}) copy-start(bf16[128,6144]{1,0:T(8,128)(2,1)} %param.13) | copy-start | bytes 4718596
  13.5 18.4 %copy-start.5 = (bf16[128,2,128]{2,1,0:T(2,128)(2,1)}, bf16[128,2,128]{2,1,0:T(2,128)(2,1)S(1)}, u32[]{:S(2)}) copy-start(bf16[128,2,128]{2,1,0:T(2,128)(2,1)S(1)} %convert_element_type.65) | copy-start | bytes 196612
  18.1 13.9 %copy-start.6 = (bf16[128,2,128]{2,1,0:T(2,128)(2,1)}, bf16[128,2,128]{2,1,0:T(2,128)(2,1)S(1)}, u32[]{:S(2)}) copy-start(bf16[128,2,128]{2,1,0:T(2,128)(2,1)S(1)} %copy.22) | copy-start | bytes 196612
  46.1 2.0 copy-start.4
  80.5 143.6 %all-reduce.6.cloned.1.call-start = ((), (), s32[]{:S(2)}) async-start(), calls=%async_computation.1 | async-start | bytes 6291456 | tf_op jit(solution)/shard_map/psum | solution.py:57
  152.3 0.7 copy-start.7
  152.4 204.8 %all-reduce.8.cloned.1.call-start = ((), (), s32[]{:S(2)}) async-start(), calls=%async_computation.2 | async-start | bytes 6291456 | tf_op jit(solution)/shard_map/psum | solution.py:63
  224.1 2.8 copy-start.3
  286.7 75.3 %copy-start.1 = (bf16[6144,256]{1,0:T(8,128)(2,1)S(1)}, bf16[6144,256]{1,0:T(8,128)(2,1)}, u32[]{:S(2)}) copy-start(bf16[6144,256]{1,0:T(8,128)(2,1)} %param.20) | copy-start | bytes 9437188
Sparse Core Ops, SparseCore 0:
  80.7 58.8 all-reduce.3
  152.5 71.5 all-reduce.5
  286.9 70.2 all-reduce.7
where the time goes:
time: 369 us
  waiting for transfers between devices  174 us (47%)
  matrix products  94.3 us (26%)
  blocking collectives  51.2 us (14%)
  other arithmetic  31 us (8%)
  between operations  14 us (4%)
  local copies, waits for them, and re-layouts  3.87 us (1%)
    psum x1, waiting for transfers between devices, local_step(): lax.psum(jnp.dot(attn_vec, w_out, preferred_element_type=jnp.float32), 'tp')  71.1 us
    psum x1, waiting for transfers between devices, local_step(): layer_out = (hidden + lax.psum(mlp_part, 'tp')).astype(jnp.bfloat16)  70.4 us
    psum x1, waiting for transfers between devices, local_step(): weighted = lax.psum(part_vals, 'sp')  32.4 us
    psum x1, blocking collectives, local_step(): denom_sum = lax.psum(jnp.sum(prob_vals, axis=-1, keepdims=True), 'sp')  25.7 us
    pmax x1, blocking collectives, local_step(): row_max = lax.pmax(jnp.max(scores, axis=-1, keepdims=True), 'sp')  25.4 us
    dot_general x1, matrix products, local_step(): mlp_part = jnp.dot(act_bf, w_down, preferred_element_type=jnp.float32)  20.5 us
    dot_general x1, matrix products, local_step(): up_proj = jnp.dot(normed_mlp, w_up, preferred_element_type=jnp.float32)  19.4 us
    dot_general x1, matrix products, local_step(): gate_pre = jnp.dot(normed_mlp, w_gate, preferred_element_type=jnp.float32)  19.3 us
  transfers between devices with their start and end apart: 3, of which 3 were waited for; matrix products, arithmetic and copies ran while one was open for 0% of the time, Pallas kernels for 0%

commit v1 on v0

v1 whole, which is shorter than its diff:
```python
import functools

import numpy as np
import jax
import jax.numpy as jnp
from jax import lax
from jax.experimental import pallas as pl
from jax.experimental.pallas import tpu as pltpu
from jax.sharding import PartitionSpec as P

ROPE_THETA = 1000000
EPS = 1e-5
NEG = -1e30
LANES = 128
HEAD_PAD = 16
WCHUNK = 256
BLK_ROWS = 16
UNROLL = 8

ANY = pl.BlockSpec(memory_space=pl.ANY)
VM = pl.BlockSpec(memory_space=pltpu.VMEM)


def attn_kernel(pos, x_ref, gain_ref, freq_ref, wq, wk, wv, kc, vc, o_out, kc_out, vc_out, kn_out, vn_out,
                xn, wbuf, kbuf, vbuf, ang, qs, kns, vns, osc, msc, lsc, wsem, csem, osem, *, blk_len, heads, kv_loc):
    rows, _ = x_ref.shape
    hd = LANES
    group = heads // kv_loc
    n_q = wq.shape[1] // WCHUNK
    per_row = blk_len * kv_loc
    n_blk = rows // BLK_ROWS
    blk_sz = BLK_ROWS * per_row

    def w_copy(i):
        if i == 0:
            src = wk
        elif i == 1:
            src = wv
        else:
            src = wq.at[:, pl.ds((i - 2) * WCHUNK, WCHUNK)]
        return pltpu.make_async_copy(src, wbuf.at[i], wsem.at[i])

    def c_in(j):
        sl = pl.ds(j * blk_sz, blk_sz)
        return (pltpu.make_async_copy(kc.at[sl], kbuf.at[sl], csem.at[2 * j]),
                pltpu.make_async_copy(vc.at[sl], vbuf.at[sl], csem.at[2 * j + 1]))

    def c_out(j):
        sl = pl.ds(j * blk_sz, blk_sz)
        return (pltpu.make_async_copy(kbuf.at[sl], kc_out.at[sl], osem.at[2 * j]),
                pltpu.make_async_copy(vbuf.at[sl], vc_out.at[sl], osem.at[2 * j + 1]))

    for i in range(n_q + 2):
        w_copy(i).start()
    for j in range(n_blk):
        for c in c_in(j):
            c.start()

    gain = gain_ref[...].astype(jnp.float32)
    for r in range(0, rows, 16):
        x = x_ref[r:r + 16, :].astype(jnp.float32)
        ms = jnp.mean(x * x, axis=-1, keepdims=True)
        xn[r:r + 16, :] = (x * lax.rsqrt(ms + EPS) * gain).astype(jnp.bfloat16)

    def ang_body(g, _):
        for u in range(8):
            b = g * 8 + u
            ang[pl.ds(b, 1), :] = pos[b].astype(jnp.float32) * freq_ref[...]
        return 0
    lax.fori_loop(0, rows // 8, ang_body, 0)
    lane = lax.broadcasted_iota(jnp.int32, (rows, hd), 1)
    even = lax.rem(lane, 2) == 0
    cos_a = jnp.cos(ang[...])
    sin_a = jnp.sin(ang[...])
    ang[...] = cos_a
    msc[0:rows, :] = jnp.where(even, -sin_a, sin_a)

    def rope(v):
        swapped = jnp.where(even, pltpu.roll(v, hd - 1, 1), pltpu.roll(v, 1, 1))
        return v * ang[...] + swapped * msc[0:rows, :]

    qs[...] = jnp.zeros(qs.shape, jnp.float32)

    w_copy(0).wait()
    res = jnp.dot(xn[...], wbuf[0], preferred_element_type=jnp.float32)
    for h in range(kv_loc):
        kns[pl.ds(h, rows, stride=kv_loc), :] = rope(res[:, h * hd:(h + 1) * hd]).astype(jnp.bfloat16).astype(jnp.float32)
    w_copy(1).wait()
    res = jnp.dot(xn[...], wbuf[1], preferred_element_type=jnp.float32)
    for h in range(kv_loc):
        vns[pl.ds(h, rows, stride=kv_loc), :] = res[:, h * hd:(h + 1) * hd].astype(jnp.bfloat16).astype(jnp.float32)
    kn_out[...] = kns[...].astype(jnp.bfloat16)
    vn_out[...] = vns[...].astype(jnp.bfloat16)

    per_w = WCHUNK // hd

    def q_body(i, _):
        pltpu.make_async_copy(wq.at[:, pl.ds(0, WCHUNK)], wbuf.at[i + 2], wsem.at[i + 2]).wait()
        r = jnp.dot(xn[...], wbuf[i + 2], preferred_element_type=jnp.float32)
        for h in range(per_w):
            qs[pl.ds(i * per_w + h, rows, stride=HEAD_PAD), :] = rope(r[:, h * hd:(h + 1) * hd])
        return 0
    lax.fori_loop(0, n_q, q_body, 0)

    base = lax.axis_index('sp') * blk_len
    s_lane = lax.broadcasted_iota(jnp.int32, (HEAD_PAD, per_row), 1)
    s_head = lax.broadcasted_iota(jnp.int32, (HEAD_PAD, per_row), 0)
    own = lax.rem(s_lane, kv_loc) == lax.div(s_head, group)
    slot_rel = jnp.where(own, lax.div(s_lane, kv_loc), 1 << 20)
    u_row = lax.broadcasted_iota(jnp.int32, (16, hd), 0)
    u_slot = lax.div(u_row, kv_loc)
    u_first = lax.rem(u_row, kv_loc) == 0
    scale = hd ** -0.5
    slots16 = 16 // kv_loc

    def blk_body(j, _):
        sl = pl.ds(pl.multiple_of(j * blk_sz, blk_sz), blk_sz)
        pltpu.make_async_copy(kc.at[sl], kbuf.at[sl], csem.at[2 * j]).wait()
        pltpu.make_async_copy(vc.at[sl], vbuf.at[sl], csem.at[2 * j + 1]).wait()

        def b_body(g, _):
            for u in range(UNROLL):
                b = j * BLK_ROWS + g * UNROLL + u
                rel = pos[b] - base
                relc = jnp.clip(rel, 0, blk_len - 1)
                grp = lax.div(relc, slots16)
                start = pl.multiple_of(b * per_row + grp * 16, 16)
                hit = u_slot == (rel - grp * slots16)
                for new, buf in ((kns, kbuf), (vns, vbuf)):
                    n0 = new[pl.ds(b * kv_loc, 1), :]
                    n1 = new[pl.ds(b * kv_loc + 1, 1), :]
                    old = buf[pl.ds(start, 16), :].astype(jnp.float32)
                    buf[pl.ds(start, 16), :] = jnp.where(hit, jnp.where(u_first, n0, n1), old).astype(jnp.bfloat16)
            for u in range(UNROLL):
                b = j * BLK_ROWS + g * UNROLL + u
                rel = pos[b] - base
                kb = kbuf[pl.ds(pl.multiple_of(b * per_row, per_row), per_row), :]
                vb = vbuf[pl.ds(pl.multiple_of(b * per_row, per_row), per_row), :]
                qb = qs[pl.ds(pl.multiple_of(b * HEAD_PAD, HEAD_PAD), HEAD_PAD), :].astype(jnp.bfloat16)
                s = lax.dot_general(qb, kb, (((1,), (1,)), ((), ())), preferred_element_type=jnp.float32) * scale
                valid = slot_rel <= rel
                s = jnp.where(valid, s, NEG)
                m = jnp.max(s, axis=-1, keepdims=True)
                w = jnp.where(valid, jnp.exp(s - m), 0.0)
                l = jnp.sum(w, axis=-1, keepdims=True)
                o = jnp.dot(w.astype(jnp.bfloat16), vb, preferred_element_type=jnp.float32)
                rs = pl.ds(pl.multiple_of(b * HEAD_PAD, HEAD_PAD), HEAD_PAD)
                osc[rs, :] = o
                msc[rs, :] = jnp.broadcast_to(m, (HEAD_PAD, hd))
                lsc[rs, :] = jnp.broadcast_to(l, (HEAD_PAD, hd))
            return 0
        lax.fori_loop(0, BLK_ROWS // UNROLL, b_body, 0)
        pltpu.make_async_copy(kbuf.at[sl], kc_out.at[sl], osem.at[2 * j]).start()
        pltpu.make_async_copy(vbuf.at[sl], vc_out.at[sl], osem.at[2 * j + 1]).start()
        return 0
    lax.fori_loop(0, n_blk, blk_body, 0)

    st = jnp.zeros((rows, hd), jnp.float32)
    for h in range(heads):
        o_out[:, h * hd:(h + 1) * hd] = osc[pl.ds(h, rows, stride=HEAD_PAD), :]
        st = jnp.where(lane == h, msc[pl.ds(h, rows, stride=HEAD_PAD), :], st)
        st = jnp.where(lane == HEAD_PAD + h, lsc[pl.ds(h, rows, stride=HEAD_PAD), :], st)
    o_out[:, heads * hd:] = st
    for j in range(n_blk):
        for c in c_out(j):
            c.wait()


def attn_call(pos, x, gain, wq, wk, wv, kc, vc, *, blk_len, heads, kv_loc):
    rows, dim = x.shape
    hd = LANES
    half = np.arange(hd) // 2
    freq = jnp.asarray((1.0 / (float(ROPE_THETA) ** (2.0 * half / hd))).astype(np.float32)).reshape(1, hd)
    n_q = wq.shape[1] // WCHUNK
    n_blk = rows // BLK_ROWS
    crow = kc.shape[0]
    f32, bf = jnp.float32, jnp.bfloat16
    return pl.pallas_call(
        functools.partial(attn_kernel, blk_len=blk_len, heads=heads, kv_loc=kv_loc),
        out_shape=(jax.ShapeDtypeStruct((rows, heads * hd + LANES), f32), jax.ShapeDtypeStruct(kc.shape, bf),
                   jax.ShapeDtypeStruct(vc.shape, bf), jax.ShapeDtypeStruct((rows * kv_loc, hd), bf),
                   jax.ShapeDtypeStruct((rows * kv_loc, hd), bf)),
        in_specs=[pl.BlockSpec(memory_space=pltpu.SMEM), VM, VM, VM, ANY, ANY, ANY, ANY, ANY],
        out_specs=(VM, ANY, ANY, VM, VM),
        scratch_shapes=[
            pltpu.VMEM((rows, dim), bf), pltpu.VMEM((n_q + 2, dim, WCHUNK), bf),
            pltpu.VMEM((crow, hd), bf), pltpu.VMEM((crow, hd), bf),
            pltpu.VMEM((rows, hd), f32), pltpu.VMEM((rows * HEAD_PAD, hd), f32),
            pltpu.VMEM((rows * kv_loc, hd), f32), pltpu.VMEM((rows * kv_loc, hd), f32),
            pltpu.VMEM((rows * HEAD_PAD, hd), f32), pltpu.VMEM((rows * HEAD_PAD, hd), f32),
            pltpu.VMEM((rows * HEAD_PAD, hd), f32),
            pltpu.SemaphoreType.DMA((n_q + 2,)), pltpu.SemaphoreType.DMA((2 * n_blk,)),
            pltpu.SemaphoreType.DMA((2 * n_blk,)),
        ],
        compiler_params=pltpu.CompilerParams(vmem_limit_bytes=60 * 1024 * 1024),
        name='attn',
    )(pos, x, gain.reshape(1, dim), freq, wq, wk, wv, kc, vc)


def rms_norm(in_vec, gain_vec):
    mean_sq = jnp.mean(jnp.square(in_vec), axis=-1, keepdims=True)
    return in_vec * lax.rsqrt(mean_sq + EPS) * gain_vec.astype(jnp.float32)


def solution(mesh):
    def local_step(layer_in, new_pos, k_blk, v_blk, attn_gain, w_query, w_key, w_value, w_out, mlp_gain, w_gate, w_up, w_down):
        num_rows = layer_in.shape[0]
        blk_len, kv_loc, head_dim = k_blk.shape[1:]
        heads = w_query.shape[1] // head_dim
        flat = (num_rows * blk_len * kv_loc, head_dim)
        part, k_upd, v_upd, k_new, v_new = attn_call(
            new_pos, layer_in, attn_gain, w_query, w_key, w_value, k_blk.reshape(flat), v_blk.reshape(flat),
            blk_len=blk_len, heads=heads, kv_loc=kv_loc)
        o_part = part[:, :heads * head_dim].reshape(num_rows, heads, head_dim)
        m_loc = part[:, heads * head_dim:heads * head_dim + heads]
        l_loc = part[:, heads * head_dim + HEAD_PAD:heads * head_dim + HEAD_PAD + heads]
        m_all = lax.pmax(m_loc, 'sp')
        fac = jnp.exp(m_loc - m_all)
        denom = lax.psum(l_loc * fac, 'sp')
        weighted = lax.psum(o_part * fac[:, :, None], 'sp')
        attn_vec = (weighted / denom[:, :, None]).reshape(num_rows, heads * head_dim).astype(jnp.bfloat16)
        x_f32 = layer_in.astype(jnp.float32)
        hidden = x_f32 + lax.psum(jnp.dot(attn_vec, w_out, preferred_element_type=jnp.float32), 'tp')
        normed_mlp = rms_norm(hidden, mlp_gain).astype(jnp.bfloat16)
        gate_pre = jnp.dot(normed_mlp, w_gate, preferred_element_type=jnp.float32)
        up_proj = jnp.dot(normed_mlp, w_up, preferred_element_type=jnp.float32)
        act_bf = (jax.nn.silu(gate_pre) * up_proj).astype(jnp.bfloat16)
        mlp_part = jnp.dot(act_bf, w_down, preferred_element_type=jnp.float32)
        layer_out = (hidden + lax.psum(mlp_part, 'tp')).astype(jnp.bfloat16)
        new_shape = (num_rows, kv_loc, head_dim)
        return layer_out, k_upd.reshape(k_blk.shape), v_upd.reshape(v_blk.shape), k_new.reshape(new_shape), v_new.reshape(new_shape)

    cache_spec = P('dp', 'sp', 'tp', None)
    new_spec = P('dp', 'tp', None)
    in_specs = (P('dp', None), P('dp'), cache_spec, cache_spec, P(None), P(None, 'tp'), P(None, 'tp'), P(None, 'tp'), P('tp', None), P(None), P(None, 'tp'), P(None, 'tp'), P('tp', None))
    out_specs = (P('dp', None), cache_spec, cache_spec, new_spec, new_spec)
    return jax.shard_map(local_step, mesh=mesh, in_specs=in_specs, out_specs=out_specs, check_vma=False)
```

time: 369 us -> 377 us (1.022)
  Pallas kernels: 0 us -> 47.5 us
  matrix products: 94.3 us -> 73 us
  other arithmetic: 31 us -> 13.2 us
    pallas_call x0 -> x1, Pallas kernels: none -> 47.5 us  [attn_call(): pl.pallas_call(functools.partial(attn_kernel, blk_len=blk_len, heads=head...]
    dot_general x5 -> x0, matrix products: 24.3 us -> none  [the longest x1 11.5 us: local_step(): jnp.dot(normed, w_query, preferred_element_type=jnp.float32)]
    select_n x1 -> x0, other arithmetic: 14.1 us -> none  [local_step(): k_upd = jnp.where(is_new, k_rot[:, None], k_blk)]
where the time goes in v1:
time: 377 us; the launch traced here: 376 us
  waiting for transfers between devices  174 us (46%)
  matrix products  73 us (19%)
  blocking collectives  49.7 us (13%)
  Pallas kernels  47.5 us (13%)
  between operations  13.8 us (4%)
  other arithmetic  13.2 us (4%)
  local copies, waits for them, and re-layouts  4.6 us (1%)
    psum x1, waiting for transfers between devices, local_step(): lax.psum(jnp.dot(attn_vec, w_out, preferred_element_type=jnp.float32), 'tp')  71.1 us
    psum x1, waiting for transfers between devices, local_step(): layer_out = (hidden + lax.psum(mlp_part, 'tp')).astype(jnp.bfloat16)  70.4 us
    pallas_call x1, Pallas kernels, attn_call(): pl.pallas_call(functools.partial(attn_kernel, blk_len=blk_len, heads=head...  47.5 us
    psum x1, waiting for transfers between devices, local_step(): weighted = lax.psum(o_part * fac[:, :, None], 'sp')  32.7 us
    psum x1, blocking collectives, local_step(): denom = lax.psum(l_loc * fac, 'sp')  25.2 us
    pmax x1, blocking collectives, local_step(): m_all = lax.pmax(m_loc, 'sp')  24.5 us
    dot_general x1, matrix products, local_step(): up_proj = jnp.dot(normed_mlp, w_up, preferred_element_type=jnp.float32)  20.8 us
    dot_general x1, matrix products, local_step(): mlp_part = jnp.dot(act_bf, w_down, preferred_element_type=jnp.float32)  20.8 us
  transfers between devices with their start and end apart: 3, of which 3 were waited for; matrix products, arithmetic and copies ran while one was open for 0% of the time, Pallas kernels for 0%

profile of v1, /device:TPU:97, one launch (start us, length us, event | category | flops | bytes accessed | tf_op | source)
XLA Modules:
  0.0 376.4 jit_solution(8065203697021897182)
XLA Ops:
  7.2 0.1 all-reduce.4.cloned.1.call-start
  7.2 1.3 reshape.50.gain_ref
  8.6 47.5 %attn.1 = (f32[128,1664]{1,0:T(8,128)}, bf16[16384,128]{1,0:T(8,128)(2,1)}, bf16[16384,128]{1,0:T(8,128)(2,1)}, bf16[256,128]{1,0:T(8,128)(2,1)}, bf16[256,128]{1,0:T(8,128)(2,1)}) custom-call(s32[128]{0:T(128)} %pos.1, bf16[128,6144]{1,0:T(8,128)(2,1)} %x_ref.1, bf16[1,6144]{1,0:T(2,128)(2,1)} %reshape.50.gain_ref, f32[1,128]{1,0:T(1,128)} %constant.15.freq_ref, ...), custom_call_target="tpu_custom_call" | custom-call | tf_op jit(solution)/shard_map/attn/pallas_call | solution.py:178
  56.1 0.8 slice.10
  57.0 1.2 slice.9
  58.1 24.5 %pmax.7 = f32[128,12]{1,0:T(8,128)S(1)} all-reduce(f32[128,12]{1,0:T(8,128)S(1)} %slice.10), channel_id=1, replica_groups=mesh['dp'=1,'tp'=4,'sp'=8] {'sp'}, use_global_device_ids=true, to_apply=%region_0.0 | all-reduce | flops 1536 | bytes 12288 | tf_op jit(solution)/shard_map/pmax | solution.py:217
  82.6 1.0 slice_multiply_fusion
  83.6 0.3 copy.19
  83.9 0.1 copy.20
  84.0 1.0 broadcast_multiply_fusion
  84.9 0.1 all-reduce.4.cloned.1.call-update
  85.0 0.1 all-reduce.6.cloned.1.call-start
  85.1 25.2 %psum.29 = f32[128,12]{1,0:T(8,128)S(1)} all-reduce(f32[128,12]{1,0:T(8,128)S(1)} %get-tuple-element.15), channel_id=1, replica_groups=mesh['dp'=1,'tp'=4,'sp'=8] {'sp'}, use_global_device_ids=true, to_apply=%region_2.0 | all-reduce | flops 1536 | bytes 12288 | tf_op jit(solution)/shard_map/psum | solution.py:219
  110.3 0.1 copy.21
  110.4 32.7 %all-reduce.4.cloned.1.call-done = f32[128,12,128]{0,2,1:T(8,128)} async-done(((f32[128,12,128]{0,2,1:T(8,128)}), f32[128,12,128]{0,2,1:T(8,128)}) %all-reduce.4.cloned.1.call-update) | async-done | bytes 786448 | tf_op jit(solution)/shard_map/psum | solution.py:220
  143.1 1.2 divide_convert_fusion
  144.3 10.8 %fusion.9 = f32[128,6144]{1,0:T(8,128)} fusion(bf16[128,1536]{0,1:T(8,128)(2,1)S(1)} %bitcast.26, bf16[1536,6144]{1,0:T(8,128)(2,1)} %param.22), kind=kOutput, calls=%fused_computation.19 | convolution fusion | flops 2415919104 | bytes 22413312 | tf_op jit(solution)/shard_map/dot_general | solution.py:223
  155.1 0.0 copy-start.1
  155.1 0.1 all-reduce.6.cloned.1.call-update
  155.2 0.1 all-reduce.8.cloned.1.call-start
  155.3 0.6 copy-done.1
  155.8 71.1 %all-reduce.6.cloned.1.call-done = f32[128,6144]{1,0:T(8,128)} async-done(((f32[128,6144]{1,0:T(8,128)}), f32[128,6144]{1,0:T(8,128)}) %all-reduce.6.cloned.1.call-update) | async-done | bytes 3145744 | tf_op jit(solution)/shard_map/psum | solution.py:223
  226.9 0.0 copy-start
  226.9 3.0 multiply_reduce_fusion
  229.9 0.3 copy-done
  230.2 3.1 multiply_convert_fusion
  233.3 20.6 %fusion.10 = f32[128,4096]{1,0:T(8,128)} fusion(bf16[128,6144]{1,0:T(8,128)(2,1)} %multiply_convert_fusion, bf16[6144,4096]{1,0:T(8,128)(2,1)} %param.24), kind=kOutput, calls=%fused_computation.20 | convolution fusion | flops 6442450944 | bytes 54001664 | tf_op jit(solution)/shard_map/dot_general | solution.py:225
  253.8 20.8 %fusion.clone.4 = bf16[128,4096]{1,0:T(8,128)(2,1)} fusion(bf16[128,6144]{1,0:T(8,128)(2,1)} %multiply_convert_fusion, bf16[6144,4096]{1,0:T(8,128)(2,1)} %param.25, f32[128,4096]{1,0:T(8,128)} %fusion.10), kind=kOutput, calls=%fused_computation.1.clone.clone.clone.1 | convolution fusion | flops 6445596672 | bytes 55050240 | tf_op jit(solution)/shard_map/dot_general | solution.py:226
  274.7 20.8 %fusion.1 = f32[128,6144]{1,0:T(8,128)} fusion(bf16[4096,6144]{1,0:T(8,128)(2,1)} %param.26, bf16[128,4096]{1,0:T(8,128)(2,1)} %fusion.clone.4), kind=kOutput, calls=%fused_computation.2 | convolution fusion | flops 6442450944 | bytes 54525952 | tf_op jit(solution)/shard_map/dot_general | solution.py:228
  295.4 0.1 all-reduce.8.cloned.1.call-update
  295.5 70.4 %all-reduce.8.cloned.1.call-done = f32[128,6144]{1,0:T(8,128)} async-done(((f32[128,6144]{1,0:T(8,128)}), f32[128,6144]{1,0:T(8,128)}) %all-reduce.8.cloned.1.call-update) | async-done | bytes 3145744 | tf_op jit(solution)/shard_map/psum | solution.py:229
  365.9 4.0 %add_convert_fusion = bf16[128,6144]{1,0:T(8,128)(2,1)} fusion(f32[128,6144]{1,0:T(8,128)} %all-reduce.8.cloned.1.call-done, f32[128,6144]{1,0:T(8,128)S(1)} %copy-done, bf16[128,6144]{1,0:T(8,128)(2,1)} %x_ref.1), kind=kLoop, calls=%fused_computation.3 | loop fusion | flops 3145728 | bytes 9437184 | tf_op jit(solution)/shard_map/convert_element_type | solution.py:229
  (2 shorter events, 0.0 us)
Async XLA Ops:
  7.2 135.9 %all-reduce.4.cloned.1.call-start = ((), (), s32[]{:S(2)}) async-start(), calls=%async_computation | async-start | bytes 1572864 | tf_op jit(solution)/shard_map/psum | solution.py:220
  85.0 141.9 %all-reduce.6.cloned.1.call-start = ((), (), s32[]{:S(2)}) async-start(), calls=%async_computation.1 | async-start | bytes 6291456 | tf_op jit(solution)/shard_map/psum | solution.py:223
  155.1 0.7 copy-start.1
  155.2 210.7 %all-reduce.8.cloned.1.call-start = ((), (), s32[]{:S(2)}) async-start(), calls=%async_computation.2 | async-start | bytes 6291456 | tf_op jit(solution)/shard_map/psum | solution.py:229
  226.9 3.3 copy-start
Sparse Core Ops, SparseCore 0:
  85.1 57.9 all-reduce.3
  155.3 71.5 all-reduce.5
  295.6 70.2 all-reduce.7

commit v2 on v1

--- a/solution.py
+++ b/solution.py
@@ -13,7 +13,7 @@
 NEG = -1e30
 LANES = 128
 HEAD_PAD = 16
-WCHUNK = 256
+KCH = 512
 BLK_ROWS = 16
 UNROLL = 8
 
@@ -22,23 +22,19 @@
 
 
 def attn_kernel(pos, x_ref, gain_ref, freq_ref, wq, wk, wv, kc, vc, o_out, kc_out, vc_out, kn_out, vn_out,
-                xn, wbuf, kbuf, vbuf, ang, qs, kns, vns, osc, msc, lsc, wsem, csem, osem, *, blk_len, heads, kv_loc):
+                xn, wqb, wkb, wvb, acc, kbuf, vbuf, ang, qs, kns, vns, osc, msc, lsc, wsem, csem, osem, *, blk_len, heads, kv_loc):
     rows, _ = x_ref.shape
     hd = LANES
     group = heads // kv_loc
-    n_q = wq.shape[1] // WCHUNK
+    n_k = wq.shape[0] // KCH
+    qw, kw = wq.shape[1], wk.shape[1]
     per_row = blk_len * kv_loc
     n_blk = rows // BLK_ROWS
     blk_sz = BLK_ROWS * per_row
 
-    def w_copy(i):
-        if i == 0:
-            src = wk
-        elif i == 1:
-            src = wv
-        else:
-            src = wq.at[:, pl.ds((i - 2) * WCHUNK, WCHUNK)]
-        return pltpu.make_async_copy(src, wbuf.at[i], wsem.at[i])
+    def w_copies(k):
+        r = pl.ds(pl.multiple_of(k * KCH, KCH), KCH)
+        return [pltpu.make_async_copy(w.at[r], buf.at[r], wsem.at[k, i]) for i, (w, buf) in enumerate(((wq, wqb), (wk, wkb), (wv, wvb)))]
 
     def c_in(j):
         sl = pl.ds(j * blk_sz, blk_sz)
@@ -50,13 +46,15 @@
         return (pltpu.make_async_copy(kbuf.at[sl], kc_out.at[sl], osem.at[2 * j]),
                 pltpu.make_async_copy(vbuf.at[sl], vc_out.at[sl], osem.at[2 * j + 1]))
 
-    for i in range(n_q + 2):
-        w_copy(i).start()
+    for k in range(n_k):
+        for cp in w_copies(k):
+            cp.start()
     for j in range(n_blk):
         for c in c_in(j):
             c.start()
 
     gain = gain_ref[...].astype(jnp.float32)
+    gain = jnp.concatenate([gain[j:j + 1, :] for j in range(gain.shape[0])], axis=1)
     for r in range(0, rows, 16):
         x = x_ref[r:r + 16, :].astype(jnp.float32)
         ms = jnp.mean(x * x, axis=-1, keepdims=True)
@@ -81,26 +79,29 @@
 
     qs[...] = jnp.zeros(qs.shape, jnp.float32)
 
-    w_copy(0).wait()
-    res = jnp.dot(xn[...], wbuf[0], preferred_element_type=jnp.float32)
+    acc[...] = jnp.zeros(acc.shape, jnp.float32)
+
+    def w_body(k, _):
+        r = pl.ds(pl.multiple_of(k * KCH, KCH), KCH)
+        cps = w_copies(k)
+        lhs = xn[:, r]
+        cps[0].wait()
+        acc[:, 0:qw] += jnp.dot(lhs, wqb[r, :], preferred_element_type=jnp.float32)
+        cps[1].wait()
+        acc[:, qw:qw + kw] += jnp.dot(lhs, wkb[r, :], preferred_element_type=jnp.float32)
+        cps[2].wait()
+        acc[:, qw + kw:] += jnp.dot(lhs, wvb[r, :], preferred_element_type=jnp.float32)
+        return 0
+    lax.fori_loop(0, n_k, w_body, 0)
     for h in range(kv_loc):
-        kns[pl.ds(h, rows, stride=kv_loc), :] = rope(res[:, h * hd:(h + 1) * hd]).astype(jnp.bfloat16).astype(jnp.float32)
-    w_copy(1).wait()
-    res = jnp.dot(xn[...], wbuf[1], preferred_element_type=jnp.float32)
-    for h in range(kv_loc):
-        vns[pl.ds(h, rows, stride=kv_loc), :] = res[:, h * hd:(h + 1) * hd].astype(jnp.bfloat16).astype(jnp.float32)
+        o = qw + h * hd
+        kns[pl.ds(h, rows, stride=kv_loc), :] = rope(acc[:, o:o + hd]).astype(jnp.bfloat16).astype(jnp.float32)
+        o = qw + kw + h * hd
+        vns[pl.ds(h, rows, stride=kv_loc), :] = acc[:, o:o + hd].astype(jnp.bfloat16).astype(jnp.float32)
     kn_out[...] = kns[...].astype(jnp.bfloat16)
     vn_out[...] = vns[...].astype(jnp.bfloat16)
-
-    per_w = WCHUNK // hd
-
-    def q_body(i, _):
-        pltpu.make_async_copy(wq.at[:, pl.ds(0, WCHUNK)], wbuf.at[i + 2], wsem.at[i + 2]).wait()
-        r = jnp.dot(xn[...], wbuf[i + 2], preferred_element_type=jnp.float32)
-        for h in range(per_w):
-            qs[pl.ds(i * per_w + h, rows, stride=HEAD_PAD), :] = rope(r[:, h * hd:(h + 1) * hd])
-        return 0
-    lax.fori_loop(0, n_q, q_body, 0)
+    for h in range(heads):
+        qs[pl.ds(h, rows, stride=HEAD_PAD), :] = rope(acc[:, h * hd:(h + 1) * hd])
 
     base = lax.axis_index('sp') * blk_len
     s_lane = lax.broadcasted_iota(jnp.int32, (HEAD_PAD, per_row), 1)
@@ -171,7 +172,7 @@
     hd = LANES
     half = np.arange(hd) // 2
     freq = jnp.asarray((1.0 / (float(ROPE_THETA) ** (2.0 * half / hd))).astype(np.float32)).reshape(1, hd)
-    n_q = wq.shape[1] // WCHUNK
+    n_k = dim // KCH
     n_blk = rows // BLK_ROWS
     crow = kc.shape[0]
     f32, bf = jnp.float32, jnp.bfloat16
@@ -183,23 +184,383 @@
         in_specs=[pl.BlockSpec(memory_space=pltpu.SMEM), VM, VM, VM, ANY, ANY, ANY, ANY, ANY],
         out_specs=(VM, ANY, ANY, VM, VM),
         scratch_shapes=[
-            pltpu.VMEM((rows, dim), bf), pltpu.VMEM((n_q + 2, dim, WCHUNK), bf),
+            pltpu.VMEM((rows, dim), bf), pltpu.VMEM(wq.shape, bf), pltpu.VMEM(wk.shape, bf), pltpu.VMEM(wv.shape, bf),
+            pltpu.VMEM((rows, wq.shape[1] + 2 * wk.shape[1]), f32),
             pltpu.VMEM((crow, hd), bf), pltpu.VMEM((crow, hd), bf),
             pltpu.VMEM((rows, hd), f32), pltpu.VMEM((rows * HEAD_PAD, hd), f32),
             pltpu.VMEM((rows * kv_loc, hd), f32), pltpu.VMEM((rows * kv_loc, hd), f32),
             pltpu.VMEM((rows * HEAD_PAD, hd), f32), pltpu.VMEM((rows * HEAD_PAD, hd), f32),
             pltpu.VMEM((rows * HEAD_PAD, hd), f32),
-            pltpu.SemaphoreType.DMA((n_q + 2,)), pltpu.SemaphoreType.DMA((2 * n_blk,)),
+            pltpu.SemaphoreType.DMA((n_k, 3)), pltpu.SemaphoreType.DMA((2 * n_blk,)),
             pltpu.SemaphoreType.DMA((2 * n_blk,)),
         ],
         compiler_params=pltpu.CompilerParams(vmem_limit_bytes=60 * 1024 * 1024),
         name='attn',
-    )(pos, x, gain.reshape(1, dim), freq, wq, wk, wv, kc, vc)
-
-
-def rms_norm(in_vec, gain_vec):
-    mean_sq = jnp.mean(jnp.square(in_vec), axis=-1, keepdims=True)
-    return in_vec * lax.rsqrt(mean_sq + EPS) * gain_vec.astype(jnp.float32)
+    )(pos, x, gain.reshape(-1, LANES), freq, wq, wk, wv, kc, vc)
+
+
+MESH = pl.DeviceIdType.MESH
+RING = 4
+CORES = 2
+PART_ROWS = 16
+OWN_ROWS = 8
+
+
+def tail_kernel(o_ref, x_hbm, gain_ref, wo, wg, wu, wd, out_ref,
+                ring_g, ring_d, ra0, ma, ra1, ra2, of, ob, p1, rb1, rb2, hb, n2, ga, ua, ab, abf, p2, rd1, rd2, yb, xs,
+                sem_g, sem_d, sem_x, send_a, recv_a, send_b, recv_b, send_c, recv_c, send_m, recv_m, send_d, recv_d,
+                send_e, recv_e, *, heads, kc):
+    f32, bf = jnp.float32, jnp.bfloat16
+    hd = LANES
+    ow = heads * hd
+    half = wo.shape[1] // CORES
+    quart = half // 2
+    fh = wg.shape[1] // CORES
+    n_g2 = ring_g.shape[0]
+    n_d = ring_d.shape[0]
+    n_wo = wo.shape[0] // kc
+    n_k = wg.shape[0] // kc
+    n_dn = wd.shape[0] // kc
+    sp = lax.axis_index('sp')
+    y = lax.axis_index('tp')
+    x = lax.div(sp, CORES)
+    c = lax.rem(sp, CORES)
+    oc = 1 - c
+
+    def xi(d):
+        return lax.rem(x + (d + RING), RING)
+
+    def yi(d):
+        return lax.rem(y + (d + RING), RING)
+
+    def xdev(d):
+        return {'sp': xi(d) * CORES + c}
+
+    def ydev(d):
+        return {'tp': yi(d)}
+
+    mate = {'sp': x * CORES + oc}
+
+    pend = []
+
+    def send(src, dst, ss, rs, dev):
+        cp = pltpu.make_async_remote_copy(src_ref=src, dst_ref=dst, send_sem=ss, recv_sem=rs, device_id=dev, device_id_type=MESH)
+        cp.start()
+        pend.append(cp)
+
+    def recv(dst, ss, rs):
+        pltpu.make_async_remote_copy(src_ref=dst, dst_ref=dst, send_sem=ss, recv_sem=rs, device_id=mate, device_id_type=MESH).wait_recv()
+
+    col_h = pl.multiple_of(c * half, half)
+    col_f = pl.multiple_of(c * fh, fh)
+
+    def g_copy(k, t):
+        w = (wg, wu)[t]
+        slot = lax.rem(k, n_g2)
+        return pltpu.make_async_copy(w.at[pl.ds(pl.multiple_of(k * kc, kc), kc), pl.ds(col_f, fh)], ring_g.at[slot, t], sem_g.at[slot, t])
+
+    def wo_copy(k):
+        return pltpu.make_async_copy(wo.at[pl.ds(pl.multiple_of(k * kc, kc), kc), pl.ds(col_h, half)], ring_d.at[lax.rem(k, n_d)], sem_d.at[lax.rem(k, n_d)])
+
+    def dn_copy(j):
+        part = lax.div(j, n_dn // 2)
+        row = lax.rem(c + part, 2) * fh + lax.rem(j, n_dn // 2) * kc
+        slot = lax.rem(j + n_wo, n_d)
+        return pltpu.make_async_copy(wd.at[pl.ds(pl.multiple_of(row, kc), kc), pl.ds(col_h, half)], ring_d.at[slot], sem_d.at[slot])
+
+    barrier = pltpu.get_barrier_semaphore()
+    for dev in (mate, xdev(1), xdev(-1), ydev(1), ydev(-1)):
+        pl.semaphore_signal(barrier, inc=1, device_id=dev, device_id_type=MESH)
+    row0 = x * (CORES * PART_ROWS) + lax.div(y, 2) * PART_ROWS
+    x_copy = pltpu.make_async_copy(x_hbm.at[pl.ds(pl.multiple_of(row0, PART_ROWS), PART_ROWS), pl.ds(col_h, half)], xs, sem_x)
+    x_copy.start()
+    for k in range(min(n_wo, n_d)):
+        wo_copy(k).start()
+    pl.semaphore_wait(barrier, 5)
+
+    for i, d in enumerate((2, 1, -1, 0)):
+        send(o_ref.at[xi(d), oc], ra0.at[i], send_a.at[i], recv_a.at[i], mate)
+    for k in range(n_g2):
+        for t in range(2):
+            g_copy(k, t).start()
+    for j in range(n_d - n_wo):
+        dn_copy(j).start()
+
+    def merge(dst, a, b, r0, nr):
+        rows = pl.ds(r0, nr)
+        sa, sb = a[rows, pl.ds(ow, LANES)], b[rows, pl.ds(ow, LANES)]
+        m = jnp.maximum(sa, sb)
+        ea, eb = jnp.exp(sa - m), jnp.exp(sb - m)
+        lane = lax.broadcasted_iota(jnp.int32, (nr, LANES), 1)
+        l = sa * pltpu.roll(ea, HEAD_PAD, 1) + sb * pltpu.roll(eb, HEAD_PAD, 1)
+        dst[rows, pl.ds(ow, LANES)] = jnp.where(lane < HEAD_PAD, m, l)
+        for h in range(heads):
+            hs = pl.ds(h * hd, hd)
+            dst[rows, hs] = a[rows, hs] * ea[:, h:h + 1] + b[rows, hs] * eb[:, h:h + 1]
+
+    R8 = OWN_ROWS
+    lo, hi = pl.ds(0, R8), pl.ds(R8, R8)
+    recv(ra0.at[0], send_a.at[0], recv_a.at[0])
+    merge(ma.at[0], o_ref.at[xi(2), c], ra0.at[0], 0, 2 * R8)
+    send(ma.at[0, lo], ra1.at[0], send_a.at[4], recv_a.at[4], xdev(1))
+    send(ma.at[0, hi], ra1.at[1], send_a.at[5], recv_a.at[5], xdev(-1))
+    recv(ra0.at[1], send_a.at[1], recv_a.at[1])
+    merge(ma.at[1], o_ref.at[xi(1), c], ra0.at[1], 0, 2 * R8)
+    send(ma.at[1, hi], ra2.at[0, hi], send_a.at[6], recv_a.at[6], xdev(1))
+    recv(ra0.at[2], send_a.at[2], recv_a.at[2])
+    merge(ma.at[2], o_ref.at[xi(-1), c], ra0.at[2], 0, 2 * R8)
+    send(ma.at[2, lo], ra2.at[1, lo], send_a.at[7], recv_a.at[7], xdev(-1))
+    recv(ra0.at[3], send_a.at[3], recv_a.at[3])
+    merge(ma.at[3], o_ref.at[xi(0), c], ra0.at[3], 0, 2 * R8)
+    recv(ra1.at[0], send_a.at[4], recv_a.at[4])
+    merge(ma.at[4, lo], ma.at[1, lo], ra1.at[0], 0, R8)
+    send(ma.at[4, lo], ra2.at[0, lo], send_a.at[8], recv_a.at[8], xdev(1))
+    recv(ra1.at[1], send_a.at[5], recv_a.at[5])
+    merge(ma.at[4, hi], ma.at[2, hi], ra1.at[1], 0, R8)
+    send(ma.at[4, hi], ra2.at[1, hi], send_a.at[9], recv_a.at[9], xdev(-1))
+    recv(ra2.at[0, hi], send_a.at[6], recv_a.at[6])
+    recv(ra2.at[1, lo], send_a.at[7], recv_a.at[7])
+    recv(ra2.at[0, lo], send_a.at[8], recv_a.at[8])
+    merge(ma.at[5], ma.at[3], ra2.at[0], 0, 2 * R8)
+    recv(ra2.at[1, hi], send_a.at[9], recv_a.at[9])
+    merge(ma.at[6], ma.at[5], ra2.at[1], 0, 2 * R8)
+    st = ma[6, :, ow:]
+    for h in range(heads):
+        hs = slice(h * hd, (h + 1) * hd)
+        of[c, :, hs] = (ma[6, :, hs] / st[:, HEAD_PAD + h:HEAD_PAD + h + 1]).astype(bf).astype(f32)
+    send(of.at[c], of.at[c], send_a.at[10], recv_a.at[10], mate)
+    recv(of.at[oc], send_a.at[10], recv_a.at[10])
+    for i in range(CORES):
+        ob[i * PART_ROWS:(i + 1) * PART_ROWS, :] = of[i].astype(bf)
+
+    p1[...] = jnp.zeros(p1.shape, f32)
+
+    def wo_body(k, _):
+        wo_copy(k).wait()
+        p1[...] += jnp.dot(ob[:, pl.ds(pl.multiple_of(k * kc, kc), kc)], ring_d[lax.rem(k, n_d)], preferred_element_type=f32)
+
+        @pl.when(k + n_d - n_wo < n_dn)
+        def _():
+            dn_copy(k + n_d - n_wo).start()
+        return 0
+    lax.fori_loop(0, n_wo, wo_body, 0)
+
+    def rs_y(p, r1, r2, ss, rs):
+        def blk(d, a):
+            return p.at[pl.ds(pl.multiple_of(yi(d) * R8, R8), R8), pl.ds(a * quart, quart)]
+        send(blk(2, 0), r1.at[0], ss.at[0], rs.at[0], ydev(1))
+        send(blk(2, 1), r1.at[1], ss.at[1], rs.at[1], ydev(-1))
+        ca, cb = pl.ds(0, quart), pl.ds(quart, quart)
+        send(blk(1, 1), r2.at[0, :, cb], ss.at[2], rs.at[2], ydev(1))
+        send(blk(-1, 0), r2.at[1, :, ca], ss.at[3], rs.at[3], ydev(-1))
+        recv(r1.at[0], ss.at[0], rs.at[0])
+        b = blk(1, 0)
+        b[...] = b[...] + r1[0]
+        send(b, r2.at[0, :, ca], ss.at[4], rs.at[4], ydev(1))
+        recv(r1.at[1], ss.at[1], rs.at[1])
+        b = blk(-1, 1)
+        b[...] = b[...] + r1[1]
+        send(b, r2.at[1, :, cb], ss.at[5], rs.at[5], ydev(-1))
+        recv(r2.at[0, :, cb], ss.at[2], rs.at[2])
+        recv(r2.at[1, :, ca], ss.at[3], rs.at[3])
+        recv(r2.at[0, :, ca], ss.at[4], rs.at[4])
+        recv(r2.at[1, :, cb], ss.at[5], rs.at[5])
+
+    own = pl.ds(pl.multiple_of(y * R8, R8), R8)
+    rs_y(p1, rb1, rb2, send_b, recv_b)
+    x_copy.wait()
+    xf = xs[...].astype(f32)
+    x8 = jnp.where(lax.rem(y, 2) == 0, xf[:R8], xf[R8:])
+    h8 = x8 + (p1[own, :] + rb2[0] + rb2[1])
+    hb[c, y, :, 0:half] = h8
+    hb[c, y, :, half:] = jnp.broadcast_to(jnp.sum(h8 * h8, axis=-1, keepdims=True), (R8, LANES))
+
+    hw = half + LANES
+    w0, w1 = pl.ds(0, quart), pl.ds(quart, hw - quart)
+    send(hb.at[c, y], hb.at[c, y], send_c.at[0], recv_c.at[0], ydev(1))
+    send(hb.at[c, y], hb.at[c, y], send_c.at[1], recv_c.at[1], ydev(-1))
+    send(hb.at[c, y], hb.at[c, y], send_c.at[4], recv_c.at[4], mate)
+    recv(hb.at[c, yi(-1)], send_c.at[0], recv_c.at[0])
+    s = hb.at[c, yi(-1), :, w0]
+    send(s, s, send_c.at[2], recv_c.at[2], ydev(1))
+    send(hb.at[c, yi(-1)], hb.at[c, yi(-1)], send_c.at[5], recv_c.at[5], mate)
+    recv(hb.at[c, yi(1)], send_c.at[1], recv_c.at[1])
+    s = hb.at[c, yi(1), :, w1]
+    send(s, s, send_c.at[3], recv_c.at[3], ydev(-1))
+    send(hb.at[c, yi(1)], hb.at[c, yi(1)], send_c.at[6], recv_c.at[6], mate)
+    recv(hb.at[c, yi(2), :, w0], send_c.at[2], recv_c.at[2])
+    recv(hb.at[c, yi(2), :, w1], send_c.at[3], recv_c.at[3])
+    send(hb.at[c, yi(2)], hb.at[c, yi(2)], send_c.at[7], recv_c.at[7], mate)
+    for i, d in enumerate((0, -1, 1, 2)):
+        recv(hb.at[oc, yi(d)], send_c.at[4 + i], recv_c.at[4 + i])
+    gain = gain_ref[...].astype(f32)
+    n_gr = half // LANES
+    for g in range(RING // 2):
+        hs = [jnp.concatenate([hb[i, 2 * g], hb[i, 2 * g + 1]], axis=0) for i in range(CORES)]
+        ssq = hs[0][:, half:half + 1] + hs[1][:, half:half + 1]
+        r = lax.rsqrt(ssq * (1.0 / (CORES * half)) + EPS)
+        for i in range(CORES):
+            gi = jnp.concatenate([gain[i * n_gr + j:i * n_gr + j + 1, :] for j in range(n_gr)], axis=1)
+            n2[g * PART_ROWS:(g + 1) * PART_ROWS, i * half:(i + 1) * half] = (hs[i][:, :half] * r * gi).astype(bf)
+
+    ga[...] = jnp.zeros(ga.shape, f32)
+    ua[...] = jnp.zeros(ua.shape, f32)
+
+    def g_body(k, _):
+        slot = lax.rem(k, n_g2)
+        lhs = n2[:, pl.ds(pl.multiple_of(k * kc, kc), kc)]
+        g_copy(k, 0).wait()
+        ga[...] += jnp.dot(lhs, ring_g[slot, 0], preferred_element_type=f32)
+        g_copy(k, 1).wait()
+        ua[...] += jnp.dot(lhs, ring_g[slot, 1], preferred_element_type=f32)
+
+        @pl.when(k + n_g2 < n_k)
+        def _():
+            g_copy(k + n_g2, 0).start()
+            g_copy(k + n_g2, 1).start()
+        return 0
+    lax.fori_loop(0, n_k, g_body, 0)
+    gp = ga[...]
+    act = (gp * jax.nn.sigmoid(gp) * ua[...]).astype(bf)
+    ab[c] = act.astype(f32)
+    send(ab.at[c], ab.at[c], send_m.at[0], recv_m.at[0], mate)
+    abf[:, 0:fh] = act
+    p2[...] = jnp.zeros(p2.shape, f32)
+
+    def dn_step(j):
+        dn_copy(j).wait()
+        p2[...] += jnp.dot(abf[:, pl.ds(pl.multiple_of(j * kc, kc), kc)], ring_d[lax.rem(j + n_wo, n_d)], preferred_element_type=f32)
+
+        @pl.when(j + n_d < n_dn)
+        def _():
+            dn_copy(j + n_d).start()
+        return 0
+    lax.fori_loop(0, n_dn // 2, lambda j, _: dn_step(j), 0)
+    recv(ab.at[oc], send_m.at[0], recv_m.at[0])
+    abf[:, fh:] = ab[oc].astype(bf)
+    lax.fori_loop(n_dn // 2, n_dn, lambda j, _: dn_step(j), 0)
+
+    rs_y(p2, rd1, rd2, send_d, recv_d)
+    y8 = hb[c, y, :, 0:half] + (p2[own, :] + rd2[0] + rd2[1])
+
+    def at(dp, dq):
+        return (lax.rem(x + (dp * oc + dq * c) + 2 * RING, RING), lax.rem(y + (dp * c + dq * oc) + 2 * RING, RING))
+
+    def piece(core, dp, dq, cols=None):
+        xx, yy = at(dp, dq)
+        return yb.at[core, xx, yy] if cols is None else yb.at[core, xx, yy, :, cols]
+
+    def pdev(d):
+        xx, yy = at(d, 0)
+        return {'sp': xx * CORES + c, 'tp': yy}
+
+    def qdev(d):
+        xx, yy = at(0, d)
+        return {'sp': xx * CORES + c, 'tp': yy}
+
+    cnt = [0]
+
+    def rsem(dp, dq, hf):
+        return recv_e.at[((dp % RING) * RING + (dq % RING)) * 2 + hf]
+
+    def esend(dp, dq, dev, rp, rq, hf, cols=None):
+        v = piece(c, dp, dq, cols)
+        send(v, v, send_e.at[cnt[0]], rsem(rp, rq, hf), dev)
+        cnt[0] += 1
+
+    def erecv(dp, dq, hf, cols=None):
+        recv(piece(c, dp, dq, cols), send_e.at[0], rsem(dp, dq, hf))
+
+    order_p = (0, -1, 1, 2)
+    ca, cb = pl.ds(0, quart), pl.ds(quart, quart)
+
+    def to_mate(dp, dq):
+        v = piece(c, dp, dq)
+        send(v, v, send_e.at[cnt[0]], recv_e.at[2 * RING * RING + (dp % RING) * RING + (dq % RING)], mate)
+        cnt[0] += 1
+
+    def q_send(dp):
+        esend(dp, 0, qdev(1), dp, -1, 0)
+        esend(dp, 0, qdev(-1), dp, 1, 0)
+
+    def q_fwd(dp):
+        erecv(dp, -1, 0)
+        esend(dp, -1, qdev(1), dp, -2, 0, ca)
+        to_mate(dp, -1)
+        erecv(dp, 1, 0)
+        esend(dp, 1, qdev(-1), dp, 2, 1, cb)
+        to_mate(dp, 1)
+
+    xx, yy = at(0, 0)
+    yb[c, xx, yy] = y8.astype(bf).astype(f32)
+    esend(0, 0, pdev(1), -1, 0, 0)
+    esend(0, 0, pdev(-1), 1, 0, 0)
+    q_send(0)
+    to_mate(0, 0)
+    erecv(-1, 0, 0)
+    esend(-1, 0, pdev(1), -2, 0, 0, ca)
+    q_send(-1)
+    to_mate(-1, 0)
+    erecv(1, 0, 0)
+    esend(1, 0, pdev(-1), 2, 0, 1, cb)
+    q_send(1)
+    to_mate(1, 0)
+    q_fwd(0)
+    erecv(2, 0, 0, ca)
+    erecv(2, 0, 1, cb)
+    q_send(2)
+    to_mate(2, 0)
+    q_fwd(-1)
+    q_fwd(1)
+    q_fwd(2)
+    for dp in order_p:
+        erecv(dp, 2, 0, ca)
+        erecv(dp, 2, 1, cb)
+        to_mate(dp, 2)
+    for dp in order_p:
+        for dq in (0, -1, 1, 2):
+            xx = lax.rem(x + (dp * c + dq * oc) + 2 * RING, RING)
+            yy = lax.rem(y + (dp * oc + dq * c) + 2 * RING, RING)
+            recv(yb.at[oc, xx, yy], send_e.at[0], recv_e.at[2 * RING * RING + (dp % RING) * RING + (dq % RING)])
+    for xx in range(RING):
+        for g in range(RING // 2):
+            r0 = xx * CORES * PART_ROWS + g * PART_ROWS
+            for i in range(CORES):
+                v = jnp.concatenate([yb[i, xx, 2 * g], yb[i, xx, 2 * g + 1]], axis=0)
+                out_ref[r0:r0 + PART_ROWS, i * half:(i + 1) * half] = v.astype(bf)
+    for cp in pend:
+        cp.wait_send()
+
+
+def tail_call(part, x, gain, wo, wg, wu, wd, *, heads, kc, n_g2, n_d):
+    rows, dim = x.shape
+    f32, bf = jnp.float32, jnp.bfloat16
+    sw = heads * LANES + LANES
+    half, fh = dim // CORES, wg.shape[1] // CORES
+    chip_rows = CORES * PART_ROWS
+    D = pltpu.SemaphoreType.DMA
+    V = pltpu.VMEM
+    n_e = 2 * RING * RING + RING * RING
+    return pl.pallas_call(
+        functools.partial(tail_kernel, heads=heads, kc=kc),
+        out_shape=jax.ShapeDtypeStruct((rows, dim), bf),
+        in_specs=[VM, ANY, VM, ANY, ANY, ANY, ANY],
+        out_specs=VM,
+        scratch_shapes=[
+            V((n_g2, 2, kc, fh), bf), V((n_d, kc, half), bf),
+            V((RING, PART_ROWS, sw), f32), V((7, PART_ROWS, sw), f32), V((2, OWN_ROWS, sw), f32), V((2, PART_ROWS, sw), f32),
+            V((CORES, PART_ROWS, heads * LANES), f32), V((chip_rows, heads * LANES), bf),
+            V((chip_rows, half), f32), V((2, OWN_ROWS, half // 2), f32), V((2, OWN_ROWS, half), f32),
+            V((CORES, RING, OWN_ROWS, half + LANES), f32), V((chip_rows, dim), bf),
+            V((chip_rows, fh), f32), V((chip_rows, fh), f32), V((CORES, chip_rows, fh), f32), V((chip_rows, CORES * fh), bf),
+            V((chip_rows, half), f32), V((2, OWN_ROWS, half // 2), f32), V((2, OWN_ROWS, half), f32),
+            V((CORES, RING, RING, OWN_ROWS, half), f32), V((PART_ROWS, half), bf),
+            D((n_g2, 2)), D((n_d,)), D(()), D((11,)), D((11,)), D((6,)), D((6,)), D((8,)), D((8,)), D((1,)), D((1,)), D((6,)), D((6,)),
+            D((40,)), D((n_e,)),
+        ],
+        compiler_params=pltpu.CompilerParams(vmem_limit_bytes=67043328, collective_id=0, has_side_effects=True),
+        name='tail',
+    )(part.reshape(rows // chip_rows, CORES, PART_ROWS, sw), x, gain.reshape(-1, LANES), wo, wg, wu, wd)
 
 
 def solution(mesh):
@@ -211,22 +572,7 @@
         part, k_upd, v_upd, k_new, v_new = attn_call(
             new_pos, layer_in, attn_gain, w_query, w_key, w_value, k_blk.reshape(flat), v_blk.reshape(flat),
             blk_len=blk_len, heads=heads, kv_loc=kv_loc)
-        o_part = part[:, :heads * head_dim].reshape(num_rows, heads, head_dim)
-        m_loc = part[:, heads * head_dim:heads * head_dim + heads]
-        l_loc = part[:, heads * head_dim + HEAD_PAD:heads * head_dim + HEAD_PAD + heads]
-        m_all = lax.pmax(m_loc, 'sp')
-        fac = jnp.exp(m_loc - m_all)
-        denom = lax.psum(l_loc * fac, 'sp')
-        weighted = lax.psum(o_part * fac[:, :, None], 'sp')
-        attn_vec = (weighted / denom[:, :, None]).reshape(num_rows, heads * head_dim).astype(jnp.bfloat16)
-        x_f32 = layer_in.astype(jnp.float32)
-        hidden = x_f32 + lax.psum(jnp.dot(attn_vec, w_out, preferred_element_type=jnp.float32), 'tp')
-        normed_mlp = rms_norm(hidden, mlp_gain).astype(jnp.bfloat16)
-        gate_pre = jnp.dot(normed_mlp, w_gate, preferred_element_type=jnp.float32)
-        up_proj = jnp.dot(normed_mlp, w_up, preferred_element_type=jnp.float32)
-        act_bf = (jax.nn.silu(gate_pre) * up_proj).astype(jnp.bfloat16)
-        mlp_part = jnp.dot(act_bf, w_down, preferred_element_type=jnp.float32)
-        layer_out = (hidden + lax.psum(mlp_part, 'tp')).astype(jnp.bfloat16)
+        layer_out = tail_call(part, layer_in, mlp_gain, w_out, w_gate, w_up, w_down, heads=heads, kc=512, n_g2=8, n_d=5)
         new_shape = (num_rows, kv_loc, head_dim)
         return layer_out, k_upd.reshape(k_blk.shape), v_upd.reshape(v_blk.shape), k_new.reshape(new_shape), v_new.reshape(new_shape)
 

time: 377 us -> 131 us (0.35)
  waiting for transfers between devices: 174 us -> 0 us
  Pallas kernels: 47.5 us -> 127 us
  matrix products: 73 us -> 0 us
  blocking collectives: 49.7 us -> 0 us
  other arithmetic: 13.2 us -> 0 us
  between operations: 13.8 us -> 0.65 us
    psum x3 -> x0, waiting for transfers between devices: 174 us -> none  [the longest x1 71.1 us: local_step(): lax.psum(jnp.dot(attn_vec, w_out, preferred_element_type=jnp.float32), 'tp')]
    pallas_call x0 -> x1, Pallas kernels: none -> 78.7 us  [tail_call(): pl.pallas_call(functools.partial(tail_kernel, heads=heads, kc=kc), out_sh...]
    dot_general x4 -> x0, matrix products: 73 us -> none  [the longest x1 20.8 us: local_step(): up_proj = jnp.dot(normed_mlp, w_up, preferred_element_type=jnp.float32)]
    psum x1 -> x0, blocking collectives: 25.2 us -> none  [local_step(): denom = lax.psum(l_loc * fac, 'sp')]
    pmax x1 -> x0, blocking collectives: 24.5 us -> none  [local_step(): m_all = lax.pmax(m_loc, 'sp')]
    convert_element_type x4 -> x0, other arithmetic: 8.24 us -> none  [the longest x1 3.96 us: local_step(): layer_out = (hidden + lax.psum(mlp_part, 'tp')).astype(jnp.bfloat16)]
  transfers between devices with their start and end apart: 3 -> 0, of which waited for: 3 -> 0; matrix products, arithmetic and copies ran while one was open for 0% -> 0% of each run, Pallas kernels for 0% -> 0%
where the time goes in v2:
time: 131 us
  Pallas kernels  127 us (97%)
  local copies, waits for them, and re-layouts  2.69 us (2%)
    pallas_call x1, Pallas kernels, tail_call(): pl.pallas_call(functools.partial(tail_kernel, heads=heads, kc=kc), out_sh...  78.7 us
    pallas_call x1, Pallas kernels, attn_call(): pl.pallas_call(functools.partial(attn_kernel, blk_len=blk_len, heads=head...  48.5 us
    unnamed x1, local copies, waits for them, and re-layouts  2.69 us

profile of v2, /device:TPU:97, one launch (start us, length us, event | category | flops | bytes accessed | tf_op | source)
XLA Modules:
  0.0 130.6 jit_solution(8303082436226647667)
XLA Ops:
  0.6 48.5 %attn.1 = (f32[128,1664]{1,0:T(8,128)}, bf16[16384,128]{1,0:T(8,128)(2,1)}, bf16[16384,128]{1,0:T(8,128)(2,1)}, bf16[256,128]{1,0:T(8,128)(2,1)}, bf16[256,128]{1,0:T(8,128)(2,1)}) custom-call(s32[128]{0:T(128)} %pos.1, bf16[128,6144]{1,0:T(8,128)(2,1)} %x_hbm.1, bf16[48,128]{1,0:T(8,128)(2,1)} %bitcast.12, f32[1,128]{1,0:T(1,128)} %constant.5.freq_ref, ...), custom_call_target="tpu_custom_call" | custom-call | tf_op jit(solution)/shard_map/attn/pallas_call | solution.py:179
  49.2 78.7 %tail.1 = bf16[128,6144]{1,0:T(8,128)(2,1)} custom-call(f32[4,2,16,1664]{3,2,1,0:T(8,128)} %bitcast.11, bf16[128,6144]{1,0:T(8,128)(2,1)} %x_hbm.1, bf16[48,128]{1,0:T(8,128)(2,1)} %bitcast.13, bf16[1536,6144]{1,0:T(8,128)(2,1)} %wo.1, bf16[6144,4096]{1,0:T(8,128)(2,1)} %wg.1, bf16[6144,4096]{1,0:T(8,128)(2,1)} %wu.1, bf16[4096,6144]{1,0:T(8,128)(2,1)} %wd.1), custom_call_target="tpu_custom_call" | custom-call | tf_op jit(solution)/shard_map/tail/pallas_call | solution.py:544
  127.9 2.7 %copy.20 = bf16[128,6144]{1,0:T(8,128)(2,1)} copy(bf16[128,6144]{1,0:T(8,128)(2,1)} %tail.1) | data formatting | bytes 3145728
